TPU v7x, 32 devices: a whole 2x2x4 slice. The times are simulated.
32 devices in a mesh: section: 4 (over z), batch: 2 (over x), tile: 4 (over y, core).
Axes of the slice: x: 2, y: 2, z: 4, core: 2. Of those that a mesh axis runs over, the one named last changes fastest.
Arguments:
- latents: bfloat16 [8, 4, 32, 1280], P('batch', 'tile'), parts along dimension 0, may hold values from -6 to 6
- prompt_tokens: bfloat16 [8, 77, 2048], P('batch'), parts along dimension 0, may hold values from -6 to 6
- fresh_noise: bfloat16 [1, 8, 4, 32, 1280], P(None, 'batch', 'tile'), parts along dimension 1, may hold values from -6 to 6
- timesteps: int32 [2], replicated, may hold values from 600 to 999
- entry_order: int32 [8], P('batch'), parts along dimension 0, may hold values from 0 to 3, each once
- timestep_weight: bfloat16 [4, 320, 1280], P('section'), may hold values from -0.3125 to 0.3125
- conv_kernel: float32 [4, 9, 1280], P('section'), may hold values from -1 to 1
- norm_gain: float32 [4, 1280], P('section'), may hold values from 0.25 to 1.75
- layer_norm_bias: float32 [4, 1280], P('section'), may hold values from -1.5 to 1.5
- qkv_weight: bfloat16 [4, 1280, 3, 1280], P('section', None, None, 'tile'), may hold values from -0.15625 to 0.15625
- prompt_weight: bfloat16 [4, 2048, 2, 1280], P('section', None, None, 'tile'), may hold values from -0.125 to 0.125
- out_weight: bfloat16 [4, 1280, 1280], P('section', 'tile'), may hold values from -0.15625 to 0.15625
Outputs:
- samples: bfloat16 [8, 4, 32, 1280], P('batch', 'tile', None, 'section'), parts along dimension 0
There are 2 independent parts, one for each index of `batch`. A program takes and returns all parts, laid end to end along the dimension named above; an argument that names none is the same for every part. Nothing has to cross between parts.
All inputs are finite; a program needn't handle non-finite values.
Results may differ from a plain program's by a relative error of at most 0.019.
Values may be sent and summed in bfloat16 or wider, within the bound.
A program may use at most 64 MiB of HBM per device.

v0:
```python
import math
import jax
import jax.numpy as jnp
from jax import lax
from jax.sharding import PartitionSpec as P

HEADS = 20


def extended(cells, sides, width):
    for axis, dim in sides:
        count = lax.axis_size(axis)
        ends = count - 1
        head = lax.slice_in_dim(cells, 0, width, axis=dim)
        tail = lax.slice_in_dim(cells, cells.shape[dim] - width, cells.shape[dim], axis=dim)
        cells = jnp.concatenate(
            [
                lax.ppermute(tail, axis, [(i, (i + 1) % count) for i in range(ends)]),
                cells,
                lax.ppermute(head, axis, [((i + 1) % count, i) for i in range(ends)]),
            ],
            axis=dim,
        )
    return cells


def from_behind(shard, axis, by):
    count = lax.axis_size(axis)
    return lax.ppermute(shard, axis, [(i, (i + by) % count) for i in range(count)])


def spread_2(shard, axis, root):
    mine = lax.axis_index(axis) == root
    return lax.psum(jnp.where(mine, shard, jnp.zeros_like(shard)), axis)


def noise_plan():
    positions = jnp.arange(1000, dtype=jnp.float32)
    low_root = math.sqrt(0.00085)
    high_root = math.sqrt(0.012)
    roots = low_root + (high_root - low_root) * positions / 999.0
    return jnp.exp(jnp.cumsum(jnp.log(1.0 - roots * roots)))


def time_features(timesteps, half_count):
    exponents = jnp.arange(half_count, dtype=jnp.float32) / half_count
    freq_row = jnp.exp(-math.log(10000.0) * exponents)
    angles = timesteps.astype(jnp.float32)[:, None] * freq_row[None, :]
    return jnp.concatenate([jnp.cos(angles), jnp.sin(angles)], axis=1).astype(jnp.bfloat16)


def pick_scalar(alpha_table, position):
    hits = jnp.arange(alpha_table.shape[0], dtype=jnp.int32) == position
    return jnp.sum(jnp.where(hits, alpha_table, jnp.zeros_like(alpha_table)))


def pick_integer(int_table, position):
    hits = jnp.arange(int_table.shape[0], dtype=jnp.int32) == position
    return jnp.sum(jnp.where(hits, int_table, jnp.zeros_like(int_table)))


def mix_positions(rimmed, kernel_body):
    row_total = rimmed.shape[0] - 2
    col_total = rimmed.shape[1]
    framed = jnp.pad(rimmed.astype(jnp.float32), ((0, 0), (1, 1), (0, 0)))
    mixed = rimmed[1:-1].astype(jnp.float32)
    for offset_row in range(3):
        for offset_col in range(3):
            mixed = (
                mixed
                + kernel_body[3 * offset_row + offset_col]
                * framed[offset_row : offset_row + row_total, offset_col : offset_col + col_total]
            )
    return mixed


def layer_norm(values_in, scale_row, shift_row):
    centre = jnp.mean(values_in, axis=-1, keepdims=True)
    spread = jnp.mean(jnp.square(values_in - centre), axis=-1, keepdims=True)
    return (values_in - centre) * lax.rsqrt(spread + 1e-05) * scale_row + shift_row


def attend(queries, keys_all, values_all, head_count):
    query_count = queries.shape[0]
    key_count = keys_all.shape[0]
    head_width = queries.shape[1] // head_count
    query_heads = queries.reshape(query_count, head_count, head_width)
    key_heads = keys_all.reshape(key_count, head_count, head_width)
    value_heads = values_all.reshape(key_count, head_count, head_width)
    scores = jnp.einsum(
        "qhd,khd->hqk", query_heads, key_heads, preferred_element_type=jnp.float32
    ) / math.sqrt(head_width)
    powers = jnp.exp(scores)
    soft_weights = (powers / jnp.sum(powers, axis=-1, keepdims=True)).astype(jnp.bfloat16)
    attended = jnp.einsum(
        "hqk,khd->qhd", soft_weights, value_heads, preferred_element_type=jnp.float32
    )
    return attended.reshape(query_count, head_count * head_width).astype(jnp.bfloat16)


def per_device(
    latents,
    prompt_tokens,
    fresh_noise,
    timesteps,
    entry_order,
    timestep_weight,
    conv_kernel,
    norm_gain,
    layer_norm_bias,
    qkv_weight,
    prompt_weight,
    out_weight,
):
    section_count = lax.axis_size("section")
    tile_count = lax.axis_size("tile")
    section_index = lax.axis_index("section")
    micro_count, rows_here, cols_here, width_all = latents.shape
    token_here = rows_here * cols_here
    chain_total = timesteps.shape[0]
    alpha_table = noise_plan()
    feature_rows = time_features(timesteps, timestep_weight.shape[1] // 2)
    timestep_embedding_all = jnp.dot(
        feature_rows, timestep_weight[0], preferred_element_type=jnp.float32
    )
    kernel_body = conv_kernel[0]
    scale_row = norm_gain[0]
    shift_row = layer_norm_bias[0]
    qkv_local = qkv_weight[0]
    prompt_local = prompt_weight[0]
    out_local = out_weight[0]
    local_heads = HEADS // tile_count
    micro_ids = jnp.arange(micro_count, dtype=jnp.int32)

    def prompt_for(latent_id):
        prompt_row = lax.dynamic_index_in_dim(prompt_tokens, latent_id, 0, False)
        local_pair = jnp.einsum(
            "tc,cjd->tjd", prompt_row, prompt_local, preferred_element_type=jnp.float32
        ).astype(jnp.bfloat16)
        return local_pair

    def lift_and_mix(current, temb_row):
        lifted = (current.astype(jnp.float32) + temb_row).astype(jnp.bfloat16)
        rimmed = extended(lifted, (("tile", 0),), 1)
        mixed = mix_positions(rimmed, kernel_body).reshape(token_here, width_all)
        normed = layer_norm(mixed, scale_row, shift_row).astype(jnp.bfloat16)
        return (mixed, normed)

    def section_heads(current, temb_row, prompt_pair):
        mixed, normed = lift_and_mix(current, temb_row)
        normed_all = lax.all_gather(normed, "tile", axis=0, tiled=True)
        projected = jnp.einsum(
            "tc,cjd->tjd", normed_all, qkv_local, preferred_element_type=jnp.float32
        ).astype(jnp.bfloat16)
        keys_all = jnp.concatenate([projected[:, 1], prompt_pair[:, 0]], axis=0)
        values_all = jnp.concatenate([projected[:, 2], prompt_pair[:, 1]], axis=0)
        attended = attend(projected[:, 0], keys_all, values_all, local_heads)
        update = lax.psum_scatter(
            jnp.dot(attended, out_local, preferred_element_type=jnp.float32).astype(jnp.bfloat16),
            "tile",
            scatter_dimension=0,
            tiled=True,
        ).astype(jnp.float32)
        return (mixed + update).astype(jnp.bfloat16).reshape(rows_here, cols_here, width_all)

    def advance(tick_counter, state_pair):
        carried_state, results = state_pair
        incoming = from_behind(carried_state, "section", 1)
        offset = tick_counter - section_index
        chain_level = jnp.floor_divide(offset, section_count)
        slot_index = offset - chain_level * section_count
        active = (offset >= 0) & (chain_level < chain_total) & (slot_index < micro_count)
        level_clip = jnp.clip(chain_level, 0, chain_total - 1)
        slot_clip = jnp.clip(slot_index, 0, micro_count - 1)
        noise_clip = jnp.clip(chain_level - 1, 0, chain_total - 2)
        latent_id = pick_integer(entry_order, slot_clip)
        starting = lax.dynamic_index_in_dim(latents, latent_id, 0, False)
        noise_slab = lax.dynamic_index_in_dim(
            lax.dynamic_index_in_dim(fresh_noise, noise_clip, 0, False), slot_clip, 0, False
        )
        alpha_bar = pick_scalar(alpha_table, pick_integer(timesteps, level_clip))
        renoised = (
            jnp.sqrt(alpha_bar) * incoming.astype(jnp.float32)
            + jnp.sqrt(1.0 - alpha_bar) * noise_slab.astype(jnp.float32)
        ).astype(jnp.bfloat16)
        first_section = section_index == 0
        current = jnp.where(
            first_section & (chain_level == 0),
            starting,
            jnp.where(first_section, renoised, incoming),
        )
        temb_row = lax.dynamic_index_in_dim(timestep_embedding_all, level_clip, 0, False)
        prompt_pair = prompt_for(latent_id)
        computed = section_heads(current, temb_row, prompt_pair)
        produced = jnp.where(active, computed, jnp.zeros_like(computed))
        finishing = active & (section_index == section_count - 1) & (chain_level == chain_total - 1)
        placing = finishing & (micro_ids == latent_id)
        results = jnp.where(placing[:, None, None, None], produced[None], results)
        return (produced, results)

    tick_total = chain_total * section_count + micro_count - 1
    initial_latent = (
        jnp.zeros((rows_here, cols_here, width_all), jnp.bfloat16),
        jnp.zeros_like(latents),
    )
    final_state = lax.fori_loop(0, tick_total, advance, initial_latent)
    gathered = spread_2(final_state[1], "section", section_count - 1)
    share_width = width_all // section_count
    return lax.dynamic_slice_in_dim(gathered, section_index * share_width, share_width, 3)


def solution(mesh):
    placed = (
        P("batch", "tile", None, None),
        P("batch", None, None),
        P(None, "batch", "tile", None, None),
        P(),
        P("batch"),
        P("section", None, None),
        P("section", None, None),
        P("section", None),
        P("section", None),
        P("section", None, None, "tile"),
        P("section", None, None, "tile"),
        P("section", "tile", None),
    )
    return jax.shard_map(
        per_device,
        mesh=mesh,
        in_specs=placed,
        out_specs=P("batch", "tile", None, "section"),
        check_vma=False,
    )
```

profile of v0, /device:TPU:0, one launch (start us, length us, event | category | flops | bytes accessed | tf_op | source)
XLA Modules:
  0.0 719.2 jit_solution(13876428785944258102)
XLA Ops:
  9.0 3.1 copy.18
  14.4 656.9 %while.18 = (s32[]{:T(128)}, bf16[1,32,1280]{2,1,0:T(8,128)(2,1)}, bf16[4,1,32,1280]{3,2,1,0:T(8,128)(2,1)}, s32[]{:T(128)}, pred[]{:T(512)}, /*index=5*/s32[4]{...) while((s32[]{:T(128)}, bf16[1,32,1280]{2,1,0:T(8,128)(2,1)}, ...), condition=%wide.region_10.11_spmd.clone, body=%wide.region_2.10_spmd.clone.sunk | while | flops 658625344 | bytes 26783188 | solution.py:206
  14.5 3.1 collective-permute-start
  32.6 3.0 collective-permute-start.2
  37.7 8.1 %all_gather.12 = bf16[128,1280]{1,0:T(8,128)(2,1)S(1)} all-gather(bf16[32,1280]{1,0:T(8,128)(2,1)S(1)} %add_convert_fusion.5), channel_id=1, replica_groups=mesh['section'=4,'batch'=2,'tile'=4] {'tile'}, dimensions={0}, use_global_device_ids=true | all-gather | bytes 409600 | tf_op jit(solution)/shard_map/while/body/eval_jaxpr/all_gather | solution.py:151
  50.0 2.3 convolution_convert_fusion.11
  52.9 19.9 %reduce-scatter.2.cloned.1.call-done = bf16[32,1280]{1,0:T(8,128)(2,1)} async-done(((bf16[128,1280]{1,0:T(8,128)(2,1)}), bf16[32,1280]{1,0:T(8,128)(2,1)}) %reduce-scatter.2.cloned.1.call-update) | async-done | bytes 81936 | tf_op jit(solution)/shard_map/while/body/eval_jaxpr/reduce_scatter | solution.py:158
  92.7 3.0 collective-permute-start.2
  97.8 7.5 %all_gather.12 = bf16[128,1280]{1,0:T(8,128)(2,1)S(1)} all-gather(bf16[32,1280]{1,0:T(8,128)(2,1)S(1)} %add_convert_fusion.5), channel_id=1, replica_groups=mesh['section'=4,'batch'=2,'tile'=4] {'tile'}, dimensions={0}, use_global_device_ids=true | all-gather | bytes 409600 | tf_op jit(solution)/shard_map/while/body/eval_jaxpr/all_gather | solution.py:151
  109.5 2.3 convolution_convert_fusion.11
  112.5 19.8 %reduce-scatter.2.cloned.1.call-done = bf16[32,1280]{1,0:T(8,128)(2,1)} async-done(((bf16[128,1280]{1,0:T(8,128)(2,1)}), bf16[32,1280]{1,0:T(8,128)(2,1)}) %reduce-scatter.2.cloned.1.call-update) | async-done | bytes 81936 | tf_op jit(solution)/shard_map/while/body/eval_jaxpr/reduce_scatter | solution.py:158
  152.3 3.0 collective-permute-start.2
  157.4 7.6 %all_gather.12 = bf16[128,1280]{1,0:T(8,128)(2,1)S(1)} all-gather(bf16[32,1280]{1,0:T(8,128)(2,1)S(1)} %add_convert_fusion.5), channel_id=1, replica_groups=mesh['section'=4,'batch'=2,'tile'=4] {'tile'}, dimensions={0}, use_global_device_ids=true | all-gather | bytes 409600 | tf_op jit(solution)/shard_map/while/body/eval_jaxpr/all_gather | solution.py:151
  169.1 2.3 convolution_convert_fusion.11
  172.1 19.8 %reduce-scatter.2.cloned.1.call-done = bf16[32,1280]{1,0:T(8,128)(2,1)} async-done(((bf16[128,1280]{1,0:T(8,128)(2,1)}), bf16[32,1280]{1,0:T(8,128)(2,1)}) %reduce-scatter.2.cloned.1.call-update) | async-done | bytes 81936 | tf_op jit(solution)/shard_map/while/body/eval_jaxpr/reduce_scatter | solution.py:158
  211.8 3.0 collective-permute-start.2
  216.9 7.6 %all_gather.12 = bf16[128,1280]{1,0:T(8,128)(2,1)S(1)} all-gather(bf16[32,1280]{1,0:T(8,128)(2,1)S(1)} %add_convert_fusion.5), channel_id=1, replica_groups=mesh['section'=4,'batch'=2,'tile'=4] {'tile'}, dimensions={0}, use_global_device_ids=true | all-gather | bytes 409600 | tf_op jit(solution)/shard_map/while/body/eval_jaxpr/all_gather | solution.py:151
  228.6 2.3 convolution_convert_fusion.11
  231.6 19.8 %reduce-scatter.2.cloned.1.call-done = bf16[32,1280]{1,0:T(8,128)(2,1)} async-done(((bf16[128,1280]{1,0:T(8,128)(2,1)}), bf16[32,1280]{1,0:T(8,128)(2,1)}) %reduce-scatter.2.cloned.1.call-update) | async-done | bytes 81936 | tf_op jit(solution)/shard_map/while/body/eval_jaxpr/reduce_scatter | solution.py:158
  271.3 3.0 collective-permute-start.2
  276.4 7.6 %all_gather.12 = bf16[128,1280]{1,0:T(8,128)(2,1)S(1)} all-gather(bf16[32,1280]{1,0:T(8,128)(2,1)S(1)} %add_convert_fusion.5), channel_id=1, replica_groups=mesh['section'=4,'batch'=2,'tile'=4] {'tile'}, dimensions={0}, use_global_device_ids=true | all-gather | bytes 409600 | tf_op jit(solution)/shard_map/while/body/eval_jaxpr/all_gather | solution.py:151
  288.1 2.3 convolution_convert_fusion.11
  291.1 19.8 %reduce-scatter.2.cloned.1.call-done = bf16[32,1280]{1,0:T(8,128)(2,1)} async-done(((bf16[128,1280]{1,0:T(8,128)(2,1)}), bf16[32,1280]{1,0:T(8,128)(2,1)}) %reduce-scatter.2.cloned.1.call-update) | async-done | bytes 81936 | tf_op jit(solution)/shard_map/while/body/eval_jaxpr/reduce_scatter | solution.py:158
  330.8 3.0 collective-permute-start.2
  335.9 7.5 %all_gather.12 = bf16[128,1280]{1,0:T(8,128)(2,1)S(1)} all-gather(bf16[32,1280]{1,0:T(8,128)(2,1)S(1)} %add_convert_fusion.5), channel_id=1, replica_groups=mesh['section'=4,'batch'=2,'tile'=4] {'tile'}, dimensions={0}, use_global_device_ids=true | all-gather | bytes 409600 | tf_op jit(solution)/shard_map/while/body/eval_jaxpr/all_gather | solution.py:151
  347.6 2.3 convolution_convert_fusion.11
  350.6 19.8 %reduce-scatter.2.cloned.1.call-done = bf16[32,1280]{1,0:T(8,128)(2,1)} async-done(((bf16[128,1280]{1,0:T(8,128)(2,1)}), bf16[32,1280]{1,0:T(8,128)(2,1)}) %reduce-scatter.2.cloned.1.call-update) | async-done | bytes 81936 | tf_op jit(solution)/shard_map/while/body/eval_jaxpr/reduce_scatter | solution.py:158
  390.3 3.0 collective-permute-start.2
  395.4 7.6 %all_gather.12 = bf16[128,1280]{1,0:T(8,128)(2,1)S(1)} all-gather(bf16[32,1280]{1,0:T(8,128)(2,1)S(1)} %add_convert_fusion.5), channel_id=1, replica_groups=mesh['section'=4,'batch'=2,'tile'=4] {'tile'}, dimensions={0}, use_global_device_ids=true | all-gather | bytes 409600 | tf_op jit(solution)/shard_map/while/body/eval_jaxpr/all_gather | solution.py:151
  407.1 2.3 convolution_convert_fusion.11
  410.1 19.8 %reduce-scatter.2.cloned.1.call-done = bf16[32,1280]{1,0:T(8,128)(2,1)} async-done(((bf16[128,1280]{1,0:T(8,128)(2,1)}), bf16[32,1280]{1,0:T(8,128)(2,1)}) %reduce-scatter.2.cloned.1.call-update) | async-done | bytes 81936 | tf_op jit(solution)/shard_map/while/body/eval_jaxpr/reduce_scatter | solution.py:158
  449.8 3.0 collective-permute-start.2
  455.0 7.5 %all_gather.12 = bf16[128,1280]{1,0:T(8,128)(2,1)S(1)} all-gather(bf16[32,1280]{1,0:T(8,128)(2,1)S(1)} %add_convert_fusion.5), channel_id=1, replica_groups=mesh['section'=4,'batch'=2,'tile'=4] {'tile'}, dimensions={0}, use_global_device_ids=true | all-gather | bytes 409600 | tf_op jit(solution)/shard_map/while/body/eval_jaxpr/all_gather | solution.py:151
  466.6 2.3 convolution_convert_fusion.11
  469.6 19.8 %reduce-scatter.2.cloned.1.call-done = bf16[32,1280]{1,0:T(8,128)(2,1)} async-done(((bf16[128,1280]{1,0:T(8,128)(2,1)}), bf16[32,1280]{1,0:T(8,128)(2,1)}) %reduce-scatter.2.cloned.1.call-update) | async-done | bytes 81936 | tf_op jit(solution)/shard_map/while/body/eval_jaxpr/reduce_scatter | solution.py:158
  509.3 3.0 collective-permute-start.2
  514.5 7.5 %all_gather.12 = bf16[128,1280]{1,0:T(8,128)(2,1)S(1)} all-gather(bf16[32,1280]{1,0:T(8,128)(2,1)S(1)} %add_convert_fusion.5), channel_id=1, replica_groups=mesh['section'=4,'batch'=2,'tile'=4] {'tile'}, dimensions={0}, use_global_device_ids=true | all-gather | bytes 409600 | tf_op jit(solution)/shard_map/while/body/eval_jaxpr/all_gather | solution.py:151
  526.2 2.3 convolution_convert_fusion.11
  529.1 19.8 %reduce-scatter.2.cloned.1.call-done = bf16[32,1280]{1,0:T(8,128)(2,1)} async-done(((bf16[128,1280]{1,0:T(8,128)(2,1)}), bf16[32,1280]{1,0:T(8,128)(2,1)}) %reduce-scatter.2.cloned.1.call-update) | async-done | bytes 81936 | tf_op jit(solution)/shard_map/while/body/eval_jaxpr/reduce_scatter | solution.py:158
  568.9 3.0 collective-permute-start.2
  574.0 7.5 %all_gather.12 = bf16[128,1280]{1,0:T(8,128)(2,1)S(1)} all-gather(bf16[32,1280]{1,0:T(8,128)(2,1)S(1)} %add_convert_fusion.5), channel_id=1, replica_groups=mesh['section'=4,'batch'=2,'tile'=4] {'tile'}, dimensions={0}, use_global_device_ids=true | all-gather | bytes 409600 | tf_op jit(solution)/shard_map/while/body/eval_jaxpr/all_gather | solution.py:151
  585.7 2.3 convolution_convert_fusion.11
  588.6 19.8 %reduce-scatter.2.cloned.1.call-done = bf16[32,1280]{1,0:T(8,128)(2,1)} async-done(((bf16[128,1280]{1,0:T(8,128)(2,1)}), bf16[32,1280]{1,0:T(8,128)(2,1)}) %reduce-scatter.2.cloned.1.call-update) | async-done | bytes 81936 | tf_op jit(solution)/shard_map/while/body/eval_jaxpr/reduce_scatter | solution.py:158
  628.4 3.0 collective-permute-start.2
  633.5 7.5 %all_gather.12 = bf16[128,1280]{1,0:T(8,128)(2,1)S(1)} all-gather(bf16[32,1280]{1,0:T(8,128)(2,1)S(1)} %add_convert_fusion.5), channel_id=1, replica_groups=mesh['section'=4,'batch'=2,'tile'=4] {'tile'}, dimensions={0}, use_global_device_ids=true | all-gather | bytes 409600 | tf_op jit(solution)/shard_map/while/body/eval_jaxpr/all_gather | solution.py:151
  645.2 2.3 convolution_convert_fusion.11
  648.1 19.8 %reduce-scatter.2.cloned.1.call-done = bf16[32,1280]{1,0:T(8,128)(2,1)} async-done(((bf16[128,1280]{1,0:T(8,128)(2,1)}), bf16[32,1280]{1,0:T(8,128)(2,1)}) %reduce-scatter.2.cloned.1.call-update) | async-done | bytes 81936 | tf_op jit(solution)/shard_map/while/body/eval_jaxpr/reduce_scatter | solution.py:158
  672.1 38.3 %all-reduce.4.cloned.1.call-done = bf16[4,1,32,1280]{3,2,1,0:T(8,128)(2,1)} async-done(((bf16[4,1,32,1280]{3,2,1,0:T(8,128)(2,1)}), bf16[4,1,32,1280]{3,2,1,0:T(8,128)(2,1)}) %all-reduce.4.cloned.1.call-update) | async-done | bytes 327696 | tf_op jit(solution)/shard_map/psum | solution.py:34
  (448 shorter events, 262.5 us)
Async XLA Ops:
  14.4 58.4 %reduce-scatter.2.cloned.1.call-start = ((), (), s32[]{:S(2)}) async-start(), calls=%async_computation.2 | async-start | bytes 409600 | tf_op jit(solution)/shard_map/while/body/eval_jaxpr/reduce_scatter | solution.py:158
  14.5 15.8 %collective-permute-start = (bf16[1,32,1280]{2,1,0:T(8,128)(2,1)}, bf16[1,32,1280]{2,1,0:T(8,128)(2,1)}, u32[]{:S(2)}, u32[]{:S(2)}) collective-permute-start(bf16[1,32,1280]{2,1,0:T(8,128)(2,1)} %get-tuple-element.768), channel_id=1, source_target_pairs={{0,8},{8,16},{16,24},{24,0},{1,9},{9,17},{17,25},{25,1},{2,10},{10... | collective-permute-start | bytes 245768 | tf_op jit(solution)/shard_map/while/body/eval_jaxpr/ppermute | solution.py:29
  31.3 5.7 collective-permute-start.1
  32.6 4.5 collective-permute-start.2
  48.4 27.8 %copy-start.6 = (f32[1,1280]{1,0:T(1,128)S(1)}, f32[1,1280]{1,0:T(1,128)}, u32[]{:S(2)}) copy-start(f32[1,1280]{1,0:T(1,128)} %get-tuple-element.859) | copy-start | bytes 15364 | tf_op jit(solution)/shard_map/while
  76.2 56.1 %reduce-scatter.2.cloned.1.call-start = ((), (), s32[]{:S(2)}) async-start(), calls=%async_computation.2 | async-start | bytes 409600 | tf_op jit(solution)/shard_map/while/body/eval_jaxpr/reduce_scatter | solution.py:158
  76.2 14.2 %collective-permute-start = (bf16[1,32,1280]{2,1,0:T(8,128)(2,1)}, bf16[1,32,1280]{2,1,0:T(8,128)(2,1)}, u32[]{:S(2)}, u32[]{:S(2)}) collective-permute-start(bf16[1,32,1280]{2,1,0:T(8,128)(2,1)} %get-tuple-element.768), channel_id=1, source_target_pairs={{0,8},{8,16},{16,24},{24,0},{1,9},{9,17},{17,25},{25,1},{2,10},{10... | collective-permute-start | bytes 245768 | tf_op jit(solution)/shard_map/while/body/eval_jaxpr/ppermute | solution.py:29
  91.4 5.7 collective-permute-start.1
  92.7 4.5 collective-permute-start.2
  108.0 27.7 %copy-start.6 = (f32[1,1280]{1,0:T(1,128)S(1)}, f32[1,1280]{1,0:T(1,128)}, u32[]{:S(2)}) copy-start(f32[1,1280]{1,0:T(1,128)} %get-tuple-element.859) | copy-start | bytes 15364 | tf_op jit(solution)/shard_map/while
  135.7 56.1 %reduce-scatter.2.cloned.1.call-start = ((), (), s32[]{:S(2)}) async-start(), calls=%async_computation.2 | async-start | bytes 409600 | tf_op jit(solution)/shard_map/while/body/eval_jaxpr/reduce_scatter | solution.py:158
  135.7 14.2 %collective-permute-start = (bf16[1,32,1280]{2,1,0:T(8,128)(2,1)}, bf16[1,32,1280]{2,1,0:T(8,128)(2,1)}, u32[]{:S(2)}, u32[]{:S(2)}) collective-permute-start(bf16[1,32,1280]{2,1,0:T(8,128)(2,1)} %get-tuple-element.768), channel_id=1, source_target_pairs={{0,8},{8,16},{16,24},{24,0},{1,9},{9,17},{17,25},{25,1},{2,10},{10... | collective-permute-start | bytes 245768 | tf_op jit(solution)/shard_map/while/body/eval_jaxpr/ppermute | solution.py:29
  151.0 5.7 collective-permute-start.1
  152.3 4.5 collective-permute-start.2
  195.3 56.1 %reduce-scatter.2.cloned.1.call-start = ((), (), s32[]{:S(2)}) async-start(), calls=%async_computation.2 | async-start | bytes 409600 | tf_op jit(solution)/shard_map/while/body/eval_jaxpr/reduce_scatter | solution.py:158
  195.3 14.1 %collective-permute-start = (bf16[1,32,1280]{2,1,0:T(8,128)(2,1)}, bf16[1,32,1280]{2,1,0:T(8,128)(2,1)}, u32[]{:S(2)}, u32[]{:S(2)}) collective-permute-start(bf16[1,32,1280]{2,1,0:T(8,128)(2,1)} %get-tuple-element.768), channel_id=1, source_target_pairs={{0,8},{8,16},{16,24},{24,0},{1,9},{9,17},{17,25},{25,1},{2,10},{10... | collective-permute-start | bytes 245768 | tf_op jit(solution)/shard_map/while/body/eval_jaxpr/ppermute | solution.py:29
  210.5 5.7 collective-permute-start.1
  211.8 4.5 collective-permute-start.2
  254.8 56.1 %reduce-scatter.2.cloned.1.call-start = ((), (), s32[]{:S(2)}) async-start(), calls=%async_computation.2 | async-start | bytes 409600 | tf_op jit(solution)/shard_map/while/body/eval_jaxpr/reduce_scatter | solution.py:158
  254.8 14.1 %collective-permute-start = (bf16[1,32,1280]{2,1,0:T(8,128)(2,1)}, bf16[1,32,1280]{2,1,0:T(8,128)(2,1)}, u32[]{:S(2)}, u32[]{:S(2)}) collective-permute-start(bf16[1,32,1280]{2,1,0:T(8,128)(2,1)} %get-tuple-element.768), channel_id=1, source_target_pairs={{0,8},{8,16},{16,24},{24,0},{1,9},{9,17},{17,25},{25,1},{2,10},{10... | collective-permute-start | bytes 245768 | tf_op jit(solution)/shard_map/while/body/eval_jaxpr/ppermute | solution.py:29
  270.0 5.7 collective-permute-start.1
  271.3 4.5 collective-permute-start.2
  314.3 56.1 %reduce-scatter.2.cloned.1.call-start = ((), (), s32[]{:S(2)}) async-start(), calls=%async_computation.2 | async-start | bytes 409600 | tf_op jit(solution)/shard_map/while/body/eval_jaxpr/reduce_scatter | solution.py:158
  314.3 14.2 %collective-permute-start = (bf16[1,32,1280]{2,1,0:T(8,128)(2,1)}, bf16[1,32,1280]{2,1,0:T(8,128)(2,1)}, u32[]{:S(2)}, u32[]{:S(2)}) collective-permute-start(bf16[1,32,1280]{2,1,0:T(8,128)(2,1)} %get-tuple-element.768), channel_id=1, source_target_pairs={{0,8},{8,16},{16,24},{24,0},{1,9},{9,17},{17,25},{25,1},{2,10},{10... | collective-permute-start | bytes 245768 | tf_op jit(solution)/shard_map/while/body/eval_jaxpr/ppermute | solution.py:29
  329.5 5.7 collective-permute-start.1
  330.8 4.5 collective-permute-start.2
  373.8 56.1 %reduce-scatter.2.cloned.1.call-start = ((), (), s32[]{:S(2)}) async-start(), calls=%async_computation.2 | async-start | bytes 409600 | tf_op jit(solution)/shard_map/while/body/eval_jaxpr/reduce_scatter | solution.py:158
  373.8 14.1 %collective-permute-start = (bf16[1,32,1280]{2,1,0:T(8,128)(2,1)}, bf16[1,32,1280]{2,1,0:T(8,128)(2,1)}, u32[]{:S(2)}, u32[]{:S(2)}) collective-permute-start(bf16[1,32,1280]{2,1,0:T(8,128)(2,1)} %get-tuple-element.768), channel_id=1, source_target_pairs={{0,8},{8,16},{16,24},{24,0},{1,9},{9,17},{17,25},{25,1},{2,10},{10... | collective-permute-start | bytes 245768 | tf_op jit(solution)/shard_map/while/body/eval_jaxpr/ppermute | solution.py:29
  389.0 5.7 collective-permute-start.1
  390.3 4.5 collective-permute-start.2
  433.3 56.1 %reduce-scatter.2.cloned.1.call-start = ((), (), s32[]{:S(2)}) async-start(), calls=%async_computation.2 | async-start | bytes 409600 | tf_op jit(solution)/shard_map/while/body/eval_jaxpr/reduce_scatter | solution.py:158
  433.3 14.2 %collective-permute-start = (bf16[1,32,1280]{2,1,0:T(8,128)(2,1)}, bf16[1,32,1280]{2,1,0:T(8,128)(2,1)}, u32[]{:S(2)}, u32[]{:S(2)}) collective-permute-start(bf16[1,32,1280]{2,1,0:T(8,128)(2,1)} %get-tuple-element.768), channel_id=1, source_target_pairs={{0,8},{8,16},{16,24},{24,0},{1,9},{9,17},{17,25},{25,1},{2,10},{10... | collective-permute-start | bytes 245768 | tf_op jit(solution)/shard_map/while/body/eval_jaxpr/ppermute | solution.py:29
  448.5 5.7 collective-permute-start.1
  449.8 4.5 collective-permute-start.2
  465.1 27.7 %copy-start.6 = (f32[1,1280]{1,0:T(1,128)S(1)}, f32[1,1280]{1,0:T(1,128)}, u32[]{:S(2)}) copy-start(f32[1,1280]{1,0:T(1,128)} %get-tuple-element.859) | copy-start | bytes 15364 | tf_op jit(solution)/shard_map/while
  492.8 56.1 %reduce-scatter.2.cloned.1.call-start = ((), (), s32[]{:S(2)}) async-start(), calls=%async_computation.2 | async-start | bytes 409600 | tf_op jit(solution)/shard_map/while/body/eval_jaxpr/reduce_scatter | solution.py:158
  492.8 14.1 %collective-permute-start = (bf16[1,32,1280]{2,1,0:T(8,128)(2,1)}, bf16[1,32,1280]{2,1,0:T(8,128)(2,1)}, u32[]{:S(2)}, u32[]{:S(2)}) collective-permute-start(bf16[1,32,1280]{2,1,0:T(8,128)(2,1)} %get-tuple-element.768), channel_id=1, source_target_pairs={{0,8},{8,16},{16,24},{24,0},{1,9},{9,17},{17,25},{25,1},{2,10},{10... | collective-permute-start | bytes 245768 | tf_op jit(solution)/shard_map/while/body/eval_jaxpr/ppermute | solution.py:29
  508.0 5.7 collective-permute-start.1
  509.3 4.5 collective-permute-start.2
  552.3 56.1 %reduce-scatter.2.cloned.1.call-start = ((), (), s32[]{:S(2)}) async-start(), calls=%async_computation.2 | async-start | bytes 409600 | tf_op jit(solution)/shard_map/while/body/eval_jaxpr/reduce_scatter | solution.py:158
  552.3 14.2 %collective-permute-start = (bf16[1,32,1280]{2,1,0:T(8,128)(2,1)}, bf16[1,32,1280]{2,1,0:T(8,128)(2,1)}, u32[]{:S(2)}, u32[]{:S(2)}) collective-permute-start(bf16[1,32,1280]{2,1,0:T(8,128)(2,1)} %get-tuple-element.768), channel_id=1, source_target_pairs={{0,8},{8,16},{16,24},{24,0},{1,9},{9,17},{17,25},{25,1},{2,10},{10... | collective-permute-start | bytes 245768 | tf_op jit(solution)/shard_map/while/body/eval_jaxpr/ppermute | solution.py:29
  567.6 5.7 collective-permute-start.1
  568.9 4.5 collective-permute-start.2
  611.8 56.1 %reduce-scatter.2.cloned.1.call-start = ((), (), s32[]{:S(2)}) async-start(), calls=%async_computation.2 | async-start | bytes 409600 | tf_op jit(solution)/shard_map/while/body/eval_jaxpr/reduce_scatter | solution.py:158
  611.8 14.1 %collective-permute-start = (bf16[1,32,1280]{2,1,0:T(8,128)(2,1)}, bf16[1,32,1280]{2,1,0:T(8,128)(2,1)}, u32[]{:S(2)}, u32[]{:S(2)}) collective-permute-start(bf16[1,32,1280]{2,1,0:T(8,128)(2,1)} %get-tuple-element.768), channel_id=1, source_target_pairs={{0,8},{8,16},{16,24},{24,0},{1,9},{9,17},{17,25},{25,1},{2,10},{10... | collective-permute-start | bytes 245768 | tf_op jit(solution)/shard_map/while/body/eval_jaxpr/ppermute | solution.py:29
  627.1 5.7 collective-permute-start.1
  628.4 4.5 collective-permute-start.2
  671.3 39.1 %all-reduce.4.cloned.1.call-start = ((), (), s32[]{:S(2)}) async-start(), calls=%async_computation.1 | async-start | bytes 655360 | tf_op jit(solution)/shard_map/psum | solution.py:34
  (36 other events, 551.4 us)
Sparse Core Ops, SparseCore 0:
  52.4 20.4 reduce-scatter.1
  111.9 20.3 reduce-scatter.1
  171.5 20.2 reduce-scatter.1
  231.0 20.2 reduce-scatter.1
  290.5 20.2 reduce-scatter.1
  350.0 20.2 reduce-scatter.1
  409.6 20.2 reduce-scatter.1
  469.1 20.3 reduce-scatter.1
  528.6 20.2 reduce-scatter.1
  588.1 20.2 reduce-scatter.1
  647.6 20.2 reduce-scatter.1
Sparse Core Ops, SparseCore 1:
  674.1 36.2 all-reduce.3
where the time goes:
time: 725 us; the launch traced here: 719 us
  waiting for transfers between devices  256 us (35%)
  other arithmetic  102 us (14%)
  matrix products  85.6 us (12%)
  blocking collectives  83.5 us (12%)
  local copies, waits for them, and re-layouts  73.6 us (10%)
  starting transfers between devices  65.6 us (9%)
  loops' own time  38.1 us (5%)
  between operations  14.6 us (2%)
    reduce_scatter x11, waiting for transfers between devices, section_heads(): lax.psum_scatter(jnp.dot(attended, out_local, preferred_element_type=jnp....  218 us
    all_gather x11, blocking collectives, section_heads(): normed_all = lax.all_gather(normed, 'tile', axis=0, tiled=True)  83.5 us
    psum x1, waiting for transfers between devices, spread_2(): return lax.psum(jnp.where(mine, shard, jnp.zeros_like(shard)), axis)  38.3 us
    another operation x1, loops' own time, per_device(): final_state = lax.fori_loop(0, tick_total, advance, initial_latent)  38.1 us
    ppermute x11, starting transfers between devices, extended(): lax.ppermute(tail, axis, [(i, (i + 1) % count) for i in range(ends)])  33.4 us
    slice x33, local copies, waits for them, and re-layouts, section_heads(): values_all = jnp.concatenate([projected[:, 2], prompt_pair[:, 1]], axis=0)  31.8 us
    dot_general x11, matrix products, section_heads(): jnp.dot(attended, out_local, preferred_element_type=jnp.float32)  24.9 us
    reduce_sum x22, other arithmetic, pick_integer(): return jnp.sum(jnp.where(hits, int_table, jnp.zeros_like(int_table)))  21.5 us
  transfers between devices with their start and end apart: 45, of which 12 were waited for; matrix products, arithmetic and copies ran while one was open for 17% of the time, Pallas kernels for 0%

commit v1 on v0

--- a/solution.py
+++ b/solution.py
@@ -148,7 +148,14 @@
 
     def section_heads(current, temb_row, prompt_pair):
         mixed, normed = lift_and_mix(current, temb_row)
-        normed_all = lax.all_gather(normed, "tile", axis=0, tiled=True)
+        ring = [normed]
+        for hop in range(3):
+            ring.append(lax.ppermute(ring[-1], "tile", [(dev, (dev + 1) % 4) for dev in range(4)]))
+        normed_all = jnp.roll(
+            jnp.concatenate(ring[::-1], axis=0),
+            (lax.axis_index("tile") + 1) * ring[0].shape[0],
+            axis=0,
+        )
         projected = jnp.einsum(
             "tc,cjd->tjd", normed_all, qkv_local, preferred_element_type=jnp.float32
         ).astype(jnp.bfloat16)

time: 725 us -> 817 us (1.13)
  blocking collectives: 83.5 us -> 0 us
  waiting for transfers between devices: 256 us -> 322 us
  local copies, waits for them, and re-layouts: 73.6 us -> 132 us
  starting transfers between devices: 65.6 us -> 95 us
  other arithmetic: 102 us -> 122 us
    all_gather x11 -> x0, blocking collectives: 83.5 us -> none  [section_heads(): normed_all = lax.all_gather(normed, 'tile', axis=0, tiled=True)]
    while x66 -> x154, local copies, waits for them, and re-layouts: 0.12 us -> 59.1 us
    ppermute x0 -> x33, waiting for transfers between devices: none -> 48.6 us  [section_heads(): lax.ppermute(ring[-1], 'tile', [(dev, (dev + 1) % 4) for dev in range(4)])]
    ppermute x0 -> x33, starting transfers between devices: none -> 29.4 us  [section_heads(): lax.ppermute(ring[-1], 'tile', [(dev, (dev + 1) % 4) for dev in range(4)])]
    reduce_scatter x11, waiting for transfers between devices: 218 us -> 235 us  [section_heads(): lax.psum_scatter(jnp.dot(attended, out_local, preferred_element_type=jnp....]
  transfers between devices with their start and end apart: 45 -> 78, of which waited for: 12 -> 34; matrix products, arithmetic and copies ran while one was open for 17% -> 16% of each run, Pallas kernels for 0% -> 0%
where the time goes in v1:
time: 817 us; the launch traced here: 808 us
  waiting for transfers between devices  322 us (39%)
  local copies, waits for them, and re-layouts  132 us (16%)
  other arithmetic  122 us (15%)
  starting transfers between devices  95 us (12%)
  matrix products  85.7 us (10%)
  loops' own time  36.2 us (4%)
  between operations  14.6 us (2%)
    reduce_scatter x11, waiting for transfers between devices, section_heads(): lax.psum_scatter(jnp.dot(attended, out_local, preferred_element_type=jnp....  235 us
    while x154, local copies, waits for them, and re-layouts  59.1 us
    ppermute x33, waiting for transfers between devices, section_heads(): lax.ppermute(ring[-1], 'tile', [(dev, (dev + 1) % 4) for dev in range(4)])  48.6 us
    psum x1, waiting for transfers between devices, spread_2(): return lax.psum(jnp.where(mine, shard, jnp.zeros_like(shard)), axis)  38.3 us
    another operation x1, loops' own time, per_device(): final_state = lax.fori_loop(0, tick_total, advance, initial_latent)  36.2 us
    ppermute x11, starting transfers between devices, extended(): lax.ppermute(tail, axis, [(i, (i + 1) % count) for i in range(ends)])  33.4 us
    slice x33, local copies, waits for them, and re-layouts, section_heads(): values_all = jnp.concatenate([projected[:, 2], prompt_pair[:, 1]], axis=0)  31.9 us
    ppermute x33, starting transfers between devices, section_heads(): lax.ppermute(ring[-1], 'tile', [(dev, (dev + 1) % 4) for dev in range(4)])  29.4 us
  transfers between devices with their start and end apart: 78, of which 34 were waited for; matrix products, arithmetic and copies ran while one was open for 16% of the time, Pallas kernels for 0%

profile of v1, /device:TPU:0, one launch (start us, length us, event | category | flops | bytes accessed | tf_op | source)
XLA Modules:
  0.0 808.1 jit_solution(14747870591438969373)
XLA Ops:
  9.0 3.1 copy.18
  14.4 745.9 %while.18 = (s32[]{:T(128)}, bf16[1,32,1280]{2,1,0:T(8,128)(2,1)}, bf16[4,1,32,1280]{3,2,1,0:T(8,128)(2,1)}, s32[]{:T(128)}, pred[]{:T(512)}, /*index=5*/s32[4]{...) while((s32[]{:T(128)}, bf16[1,32,1280]{2,1,0:T(8,128)(2,1)}, ...), condition=%wide.region_10.11_spmd.clone, body=%wide.region_2.10_spmd.clone.sunk | while | flops 659035008 | bytes 29193816 | solution.py:213
  14.4 3.1 collective-permute-start
  27.8 3.0 collective-permute-start.2
  34.2 2.7 collective-permute-done.3
  56.6 2.3 convolution_convert_fusion.11
  59.5 21.5 %reduce-scatter.2.cloned.1.call-done = bf16[32,1280]{1,0:T(8,128)(2,1)} async-done(((bf16[128,1280]{1,0:T(8,128)(2,1)}), bf16[32,1280]{1,0:T(8,128)(2,1)}) %reduce-scatter.2.cloned.1.call-update) | async-done | bytes 81936 | tf_op jit(solution)/shard_map/while/body/eval_jaxpr/reduce_scatter | solution.py:165
  96.1 3.0 collective-permute-start.2
  101.9 3.2 collective-permute-done.3
  124.4 2.3 convolution_convert_fusion.11
  127.2 21.3 %reduce-scatter.2.cloned.1.call-done = bf16[32,1280]{1,0:T(8,128)(2,1)} async-done(((bf16[128,1280]{1,0:T(8,128)(2,1)}), bf16[32,1280]{1,0:T(8,128)(2,1)}) %reduce-scatter.2.cloned.1.call-update) | async-done | bytes 81936 | tf_op jit(solution)/shard_map/while/body/eval_jaxpr/reduce_scatter | solution.py:165
  163.7 3.0 collective-permute-start.2
  169.5 3.2 collective-permute-done.3
  192.0 2.3 convolution_convert_fusion.11
  194.8 21.3 %reduce-scatter.2.cloned.1.call-done = bf16[32,1280]{1,0:T(8,128)(2,1)} async-done(((bf16[128,1280]{1,0:T(8,128)(2,1)}), bf16[32,1280]{1,0:T(8,128)(2,1)}) %reduce-scatter.2.cloned.1.call-update) | async-done | bytes 81936 | tf_op jit(solution)/shard_map/while/body/eval_jaxpr/reduce_scatter | solution.py:165
  231.3 3.0 collective-permute-start.2
  237.1 3.2 collective-permute-done.3
  259.5 2.3 convolution_convert_fusion.11
  262.4 21.3 %reduce-scatter.2.cloned.1.call-done = bf16[32,1280]{1,0:T(8,128)(2,1)} async-done(((bf16[128,1280]{1,0:T(8,128)(2,1)}), bf16[32,1280]{1,0:T(8,128)(2,1)}) %reduce-scatter.2.cloned.1.call-update) | async-done | bytes 81936 | tf_op jit(solution)/shard_map/while/body/eval_jaxpr/reduce_scatter | solution.py:165
  298.9 3.0 collective-permute-start.2
  304.7 3.2 collective-permute-done.3
  327.1 2.3 convolution_convert_fusion.11
  330.0 21.3 %reduce-scatter.2.cloned.1.call-done = bf16[32,1280]{1,0:T(8,128)(2,1)} async-done(((bf16[128,1280]{1,0:T(8,128)(2,1)}), bf16[32,1280]{1,0:T(8,128)(2,1)}) %reduce-scatter.2.cloned.1.call-update) | async-done | bytes 81936 | tf_op jit(solution)/shard_map/while/body/eval_jaxpr/reduce_scatter | solution.py:165
  366.5 3.0 collective-permute-start.2
  372.3 3.2 collective-permute-done.3
  394.7 2.3 convolution_convert_fusion.11
  397.6 21.3 %reduce-scatter.2.cloned.1.call-done = bf16[32,1280]{1,0:T(8,128)(2,1)} async-done(((bf16[128,1280]{1,0:T(8,128)(2,1)}), bf16[32,1280]{1,0:T(8,128)(2,1)}) %reduce-scatter.2.cloned.1.call-update) | async-done | bytes 81936 | tf_op jit(solution)/shard_map/while/body/eval_jaxpr/reduce_scatter | solution.py:165
  434.1 3.0 collective-permute-start.2
  439.9 3.2 collective-permute-done.3
  462.3 2.3 convolution_convert_fusion.11
  465.2 21.3 %reduce-scatter.2.cloned.1.call-done = bf16[32,1280]{1,0:T(8,128)(2,1)} async-done(((bf16[128,1280]{1,0:T(8,128)(2,1)}), bf16[32,1280]{1,0:T(8,128)(2,1)}) %reduce-scatter.2.cloned.1.call-update) | async-done | bytes 81936 | tf_op jit(solution)/shard_map/while/body/eval_jaxpr/reduce_scatter | solution.py:165
  501.7 3.0 collective-permute-start.2
  507.5 3.2 collective-permute-done.3
  530.0 2.3 convolution_convert_fusion.11
  532.8 21.3 %reduce-scatter.2.cloned.1.call-done = bf16[32,1280]{1,0:T(8,128)(2,1)} async-done(((bf16[128,1280]{1,0:T(8,128)(2,1)}), bf16[32,1280]{1,0:T(8,128)(2,1)}) %reduce-scatter.2.cloned.1.call-update) | async-done | bytes 81936 | tf_op jit(solution)/shard_map/while/body/eval_jaxpr/reduce_scatter | solution.py:165
  569.3 3.0 collective-permute-start.2
  575.1 3.2 collective-permute-done.3
  597.5 2.3 convolution_convert_fusion.11
  600.4 21.3 %reduce-scatter.2.cloned.1.call-done = bf16[32,1280]{1,0:T(8,128)(2,1)} async-done(((bf16[128,1280]{1,0:T(8,128)(2,1)}), bf16[32,1280]{1,0:T(8,128)(2,1)}) %reduce-scatter.2.cloned.1.call-update) | async-done | bytes 81936 | tf_op jit(solution)/shard_map/while/body/eval_jaxpr/reduce_scatter | solution.py:165
  636.9 3.0 collective-permute-start.2
  642.7 3.2 collective-permute-done.3
  665.1 2.3 convolution_convert_fusion.11
  668.0 21.3 %reduce-scatter.2.cloned.1.call-done = bf16[32,1280]{1,0:T(8,128)(2,1)} async-done(((bf16[128,1280]{1,0:T(8,128)(2,1)}), bf16[32,1280]{1,0:T(8,128)(2,1)}) %reduce-scatter.2.cloned.1.call-update) | async-done | bytes 81936 | tf_op jit(solution)/shard_map/while/body/eval_jaxpr/reduce_scatter | solution.py:165
  704.5 3.0 collective-permute-start.2
  710.3 3.2 collective-permute-done.3
  732.7 2.3 convolution_convert_fusion.11
  735.6 21.3 %reduce-scatter.2.cloned.1.call-done = bf16[32,1280]{1,0:T(8,128)(2,1)} async-done(((bf16[128,1280]{1,0:T(8,128)(2,1)}), bf16[32,1280]{1,0:T(8,128)(2,1)}) %reduce-scatter.2.cloned.1.call-update) | async-done | bytes 81936 | tf_op jit(solution)/shard_map/while/body/eval_jaxpr/reduce_scatter | solution.py:165
  761.0 38.3 %all-reduce.4.cloned.1.call-done = bf16[4,1,32,1280]{3,2,1,0:T(8,128)(2,1)} async-done(((bf16[4,1,32,1280]{3,2,1,0:T(8,128)(2,1)}), bf16[4,1,32,1280]{3,2,1,0:T(8,128)(2,1)}) %all-reduce.4.cloned.1.call-update) | async-done | bytes 327696 | tf_op jit(solution)/shard_map/psum | solution.py:34
  (611 shorter events, 385.6 us)
Async XLA Ops:
  14.4 66.7 %reduce-scatter.2.cloned.1.call-start = ((), (), s32[]{:S(2)}) async-start(), calls=%async_computation.2 | async-start | bytes 409600 | tf_op jit(solution)/shard_map/while/body/eval_jaxpr/reduce_scatter | solution.py:165
  14.4 11.1 %collective-permute-start = (bf16[1,32,1280]{2,1,0:T(8,128)(2,1)}, bf16[1,32,1280]{2,1,0:T(8,128)(2,1)S(1)}, u32[]{:S(2)}, u32[]{:S(2)}) collective-permute-start(bf16[1,32,1280]{2,1,0:T(8,128)(2,1)} %get-tuple-element.776), channel_id=1, source_target_pairs={{0,8},{8,16},{16,24},{24,0},{1,9},{9,17},{17,25},{25,1},{2,10},{10... | collective-permute-start | bytes 245768 | tf_op jit(solution)/shard_map/while/body/eval_jaxpr/ppermute | solution.py:29
  26.5 5.7 collective-permute-start.1
  27.8 4.4 collective-permute-start.2
  40.8 4.8 collective-permute-start.5
  84.3 64.2 %reduce-scatter.2.cloned.1.call-start = ((), (), s32[]{:S(2)}) async-start(), calls=%async_computation.2 | async-start | bytes 409600 | tf_op jit(solution)/shard_map/while/body/eval_jaxpr/reduce_scatter | solution.py:165
  84.3 9.5 %collective-permute-start = (bf16[1,32,1280]{2,1,0:T(8,128)(2,1)}, bf16[1,32,1280]{2,1,0:T(8,128)(2,1)S(1)}, u32[]{:S(2)}, u32[]{:S(2)}) collective-permute-start(bf16[1,32,1280]{2,1,0:T(8,128)(2,1)} %get-tuple-element.776), channel_id=1, source_target_pairs={{0,8},{8,16},{16,24},{24,0},{1,9},{9,17},{17,25},{25,1},{2,10},{10... | collective-permute-start | bytes 245768 | tf_op jit(solution)/shard_map/while/body/eval_jaxpr/ppermute | solution.py:29
  94.8 5.7 collective-permute-start.1
  96.1 4.4 collective-permute-start.2
  109.1 4.3 collective-permute-start.5
  151.9 64.2 %reduce-scatter.2.cloned.1.call-start = ((), (), s32[]{:S(2)}) async-start(), calls=%async_computation.2 | async-start | bytes 409600 | tf_op jit(solution)/shard_map/while/body/eval_jaxpr/reduce_scatter | solution.py:165
  151.9 9.5 %collective-permute-start = (bf16[1,32,1280]{2,1,0:T(8,128)(2,1)}, bf16[1,32,1280]{2,1,0:T(8,128)(2,1)S(1)}, u32[]{:S(2)}, u32[]{:S(2)}) collective-permute-start(bf16[1,32,1280]{2,1,0:T(8,128)(2,1)} %get-tuple-element.776), channel_id=1, source_target_pairs={{0,8},{8,16},{16,24},{24,0},{1,9},{9,17},{17,25},{25,1},{2,10},{10... | collective-permute-start | bytes 245768 | tf_op jit(solution)/shard_map/while/body/eval_jaxpr/ppermute | solution.py:29
  162.4 5.7 collective-permute-start.1
  163.7 4.4 collective-permute-start.2
  219.5 64.2 %reduce-scatter.2.cloned.1.call-start = ((), (), s32[]{:S(2)}) async-start(), calls=%async_computation.2 | async-start | bytes 409600 | tf_op jit(solution)/shard_map/while/body/eval_jaxpr/reduce_scatter | solution.py:165
  219.5 9.5 %collective-permute-start = (bf16[1,32,1280]{2,1,0:T(8,128)(2,1)}, bf16[1,32,1280]{2,1,0:T(8,128)(2,1)S(1)}, u32[]{:S(2)}, u32[]{:S(2)}) collective-permute-start(bf16[1,32,1280]{2,1,0:T(8,128)(2,1)} %get-tuple-element.776), channel_id=1, source_target_pairs={{0,8},{8,16},{16,24},{24,0},{1,9},{9,17},{17,25},{25,1},{2,10},{10... | collective-permute-start | bytes 245768 | tf_op jit(solution)/shard_map/while/body/eval_jaxpr/ppermute | solution.py:29
  230.0 5.7 collective-permute-start.1
  231.3 4.4 collective-permute-start.2
  287.1 64.3 %reduce-scatter.2.cloned.1.call-start = ((), (), s32[]{:S(2)}) async-start(), calls=%async_computation.2 | async-start | bytes 409600 | tf_op jit(solution)/shard_map/while/body/eval_jaxpr/reduce_scatter | solution.py:165
  287.1 9.5 %collective-permute-start = (bf16[1,32,1280]{2,1,0:T(8,128)(2,1)}, bf16[1,32,1280]{2,1,0:T(8,128)(2,1)S(1)}, u32[]{:S(2)}, u32[]{:S(2)}) collective-permute-start(bf16[1,32,1280]{2,1,0:T(8,128)(2,1)} %get-tuple-element.776), channel_id=1, source_target_pairs={{0,8},{8,16},{16,24},{24,0},{1,9},{9,17},{17,25},{25,1},{2,10},{10... | collective-permute-start | bytes 245768 | tf_op jit(solution)/shard_map/while/body/eval_jaxpr/ppermute | solution.py:29
  297.6 5.7 collective-permute-start.1
  298.9 4.4 collective-permute-start.2
  354.7 64.2 %reduce-scatter.2.cloned.1.call-start = ((), (), s32[]{:S(2)}) async-start(), calls=%async_computation.2 | async-start | bytes 409600 | tf_op jit(solution)/shard_map/while/body/eval_jaxpr/reduce_scatter | solution.py:165
  354.7 9.5 %collective-permute-start = (bf16[1,32,1280]{2,1,0:T(8,128)(2,1)}, bf16[1,32,1280]{2,1,0:T(8,128)(2,1)S(1)}, u32[]{:S(2)}, u32[]{:S(2)}) collective-permute-start(bf16[1,32,1280]{2,1,0:T(8,128)(2,1)} %get-tuple-element.776), channel_id=1, source_target_pairs={{0,8},{8,16},{16,24},{24,0},{1,9},{9,17},{17,25},{25,1},{2,10},{10... | collective-permute-start | bytes 245768 | tf_op jit(solution)/shard_map/while/body/eval_jaxpr/ppermute | solution.py:29
  365.2 5.7 collective-permute-start.1
  366.5 4.4 collective-permute-start.2
  422.3 64.2 %reduce-scatter.2.cloned.1.call-start = ((), (), s32[]{:S(2)}) async-start(), calls=%async_computation.2 | async-start | bytes 409600 | tf_op jit(solution)/shard_map/while/body/eval_jaxpr/reduce_scatter | solution.py:165
  422.3 9.5 %collective-permute-start = (bf16[1,32,1280]{2,1,0:T(8,128)(2,1)}, bf16[1,32,1280]{2,1,0:T(8,128)(2,1)S(1)}, u32[]{:S(2)}, u32[]{:S(2)}) collective-permute-start(bf16[1,32,1280]{2,1,0:T(8,128)(2,1)} %get-tuple-element.776), channel_id=1, source_target_pairs={{0,8},{8,16},{16,24},{24,0},{1,9},{9,17},{17,25},{25,1},{2,10},{10... | collective-permute-start | bytes 245768 | tf_op jit(solution)/shard_map/while/body/eval_jaxpr/ppermute | solution.py:29
  432.8 5.7 collective-permute-start.1
  434.1 4.4 collective-permute-start.2
  489.9 64.2 %reduce-scatter.2.cloned.1.call-start = ((), (), s32[]{:S(2)}) async-start(), calls=%async_computation.2 | async-start | bytes 409600 | tf_op jit(solution)/shard_map/while/body/eval_jaxpr/reduce_scatter | solution.py:165
  489.9 9.5 %collective-permute-start = (bf16[1,32,1280]{2,1,0:T(8,128)(2,1)}, bf16[1,32,1280]{2,1,0:T(8,128)(2,1)S(1)}, u32[]{:S(2)}, u32[]{:S(2)}) collective-permute-start(bf16[1,32,1280]{2,1,0:T(8,128)(2,1)} %get-tuple-element.776), channel_id=1, source_target_pairs={{0,8},{8,16},{16,24},{24,0},{1,9},{9,17},{17,25},{25,1},{2,10},{10... | collective-permute-start | bytes 245768 | tf_op jit(solution)/shard_map/while/body/eval_jaxpr/ppermute | solution.py:29
  500.4 5.7 collective-permute-start.1
  501.7 4.4 collective-permute-start.2
  557.5 64.3 %reduce-scatter.2.cloned.1.call-start = ((), (), s32[]{:S(2)}) async-start(), calls=%async_computation.2 | async-start | bytes 409600 | tf_op jit(solution)/shard_map/while/body/eval_jaxpr/reduce_scatter | solution.py:165
  557.5 9.5 %collective-permute-start = (bf16[1,32,1280]{2,1,0:T(8,128)(2,1)}, bf16[1,32,1280]{2,1,0:T(8,128)(2,1)S(1)}, u32[]{:S(2)}, u32[]{:S(2)}) collective-permute-start(bf16[1,32,1280]{2,1,0:T(8,128)(2,1)} %get-tuple-element.776), channel_id=1, source_target_pairs={{0,8},{8,16},{16,24},{24,0},{1,9},{9,17},{17,25},{25,1},{2,10},{10... | collective-permute-start | bytes 245768 | tf_op jit(solution)/shard_map/while/body/eval_jaxpr/ppermute | solution.py:29
  568.0 5.7 collective-permute-start.1
  569.3 4.4 collective-permute-start.2
  625.1 64.2 %reduce-scatter.2.cloned.1.call-start = ((), (), s32[]{:S(2)}) async-start(), calls=%async_computation.2 | async-start | bytes 409600 | tf_op jit(solution)/shard_map/while/body/eval_jaxpr/reduce_scatter | solution.py:165
  625.1 9.5 %collective-permute-start = (bf16[1,32,1280]{2,1,0:T(8,128)(2,1)}, bf16[1,32,1280]{2,1,0:T(8,128)(2,1)S(1)}, u32[]{:S(2)}, u32[]{:S(2)}) collective-permute-start(bf16[1,32,1280]{2,1,0:T(8,128)(2,1)} %get-tuple-element.776), channel_id=1, source_target_pairs={{0,8},{8,16},{16,24},{24,0},{1,9},{9,17},{17,25},{25,1},{2,10},{10... | collective-permute-start | bytes 245768 | tf_op jit(solution)/shard_map/while/body/eval_jaxpr/ppermute | solution.py:29
  635.6 5.7 collective-permute-start.1
  636.9 4.4 collective-permute-start.2
  692.7 64.3 %reduce-scatter.2.cloned.1.call-start = ((), (), s32[]{:S(2)}) async-start(), calls=%async_computation.2 | async-start | bytes 409600 | tf_op jit(solution)/shard_map/while/body/eval_jaxpr/reduce_scatter | solution.py:165
  692.7 9.5 %collective-permute-start = (bf16[1,32,1280]{2,1,0:T(8,128)(2,1)}, bf16[1,32,1280]{2,1,0:T(8,128)(2,1)S(1)}, u32[]{:S(2)}, u32[]{:S(2)}) collective-permute-start(bf16[1,32,1280]{2,1,0:T(8,128)(2,1)} %get-tuple-element.776), channel_id=1, source_target_pairs={{0,8},{8,16},{16,24},{24,0},{1,9},{9,17},{17,25},{25,1},{2,10},{10... | collective-permute-start | bytes 245768 | tf_op jit(solution)/shard_map/while/body/eval_jaxpr/ppermute | solution.py:29
  703.2 5.7 collective-permute-start.1
  704.5 4.4 collective-permute-start.2
  717.4 4.3 collective-permute-start.5
  760.3 39.1 %all-reduce.4.cloned.1.call-start = ((), (), s32[]{:S(2)}) async-start(), calls=%async_computation.1 | async-start | bytes 655360 | tf_op jit(solution)/shard_map/psum | solution.py:34
  (79 other events, 731.5 us)
Sparse Core Ops, SparseCore 0:
  59.0 21.9 reduce-scatter.1
  126.8 21.7 reduce-scatter.1
  194.4 21.7 reduce-scatter.1
  261.9 21.7 reduce-scatter.1
  329.5 21.7 reduce-scatter.1
  397.2 21.7 reduce-scatter.1
  464.7 21.7 reduce-scatter.1
  532.4 21.7 reduce-scatter.1
  599.9 21.7 reduce-scatter.1
  667.5 21.7 reduce-scatter.1
  735.1 21.7 reduce-scatter.1
Sparse Core Ops, SparseCore 1:
  763.1 36.2 all-reduce.3
